TPU v7x, 32 devices: a whole 2x2x4 slice. The times are simulated.
32 devices in a mesh: dp: 4 (over y, x), vocab: 8 (over z, core).
Axes of the slice: x: 2, y: 2, z: 4, core: 2. Of those that a mesh axis runs over, the one named last changes fastest.
Arguments:
- hidden: bfloat16 [4, 32, 3584], P('dp', None, 'vocab'), may hold values from -6 to 6
- kl_hidden: bfloat16 [4, 32, 3584], P('dp', None, 'vocab'), may hold values from -6 to 6
- head_weight: bfloat16 [256000, 3584], P(('dp', 'vocab')), may hold values from -0.3125 to 0.3125
- labels: int32 [4, 32], P('dp'), may hold values from 0 to 255999
- token_mask: int32 [4, 32], P('dp'), may hold values 0 or 1
- kl_pair: int32 [4], P('dp'), may hold values from 0 to 3, as said below
- desirable: int32 [4], P('dp'), may hold values 0 or 1
- ref_logps: float32 [4, 64], P('dp', 'vocab'), may hold values from -23 to -11
Outputs:
- token_logps: float32 [4, 64], P('dp', 'vocab')
- seq_losses: float32 [4], P('dp')
- loss: float32 [], replicated
Inputs may be any that keep to these rules, and one draw needn't show every extreme that they name: kl_pair is a permutation of the 4 sequences with kl_pair[s] != s.
All inputs are finite; a program needn't handle non-finite values. No bound on the sum of `token_mask` or of `desirable` on one device may be relied on, other than what follows from the above.
Results may differ from a plain program's by a relative error of at most 0.0003.
Values may be sent and summed in bfloat16 or wider, within the bound.
A program may use at most 128 MiB of HBM per device.

v0:
```python
import jax
import jax.numpy as jnp
from jax import lax
from jax.sharding import PartitionSpec as P

kto_beta = 0.1
desirable_weight = 1.0
undesirable_weight = 1.33


def label_terms(logits, targets, first_row):
    shifted = targets - first_row
    inside = (shifted >= 0) & (shifted < logits.shape[1])
    clipped = jnp.clip(shifted, 0, logits.shape[1] - 1)
    picked = jnp.take_along_axis(logits, clipped[:, None], axis=1)[:, 0]
    return (jnp.sum(jnp.exp(logits), axis=1), jnp.where(inside, picked, 0.0))


def kto_losses(logratio, kl_total, seq_total, desirable):
    kl_estimate = kl_total / seq_total
    wanted = desirable_weight * (1.0 - jax.nn.sigmoid(kto_beta * (logratio - kl_estimate)))
    unwanted = undesirable_weight * (1.0 - jax.nn.sigmoid(kto_beta * (kl_estimate - logratio)))
    return jnp.where(desirable == 1, wanted, unwanted)


def on_device(hidden, kl_hidden, head_weight, labels, token_mask, kl_pair, desirable, ref_logps):
    sub_seq = hidden.shape[0]
    length = hidden.shape[1]
    vocab_rows = head_weight.shape[0]
    model_width = head_weight.shape[1]
    groups = lax.axis_size("vocab")
    vocab_index = lax.axis_index("vocab")
    data_index = lax.axis_index("dp")
    first_row = (data_index * groups + vocab_index) * vocab_rows
    all_labels, all_masks, all_pairs, all_desirable = (
        lax.all_gather(labels, "dp", axis=0, tiled=True),
        lax.all_gather(token_mask, "dp", axis=0, tiled=True),
        lax.all_gather(kl_pair, "dp", axis=0, tiled=True),
        lax.all_gather(desirable, "dp", axis=0, tiled=True),
    )
    targets = jnp.concatenate([all_labels, all_labels[all_pairs]], axis=1)
    weights_mask = jnp.concatenate([all_masks, all_masks[all_pairs]], axis=1).astype(jnp.float32)
    seq_total = targets.shape[0]
    columns = targets.shape[1]
    combined = jnp.concatenate([hidden, kl_hidden], axis=1)
    whole_rows = lax.all_gather(combined, "vocab", axis=2, tiled=True)
    portion = lax.all_gather(whole_rows, "dp", axis=0, tiled=True)
    number = portion.shape[0]
    logits = lax.dot_general(
        portion.reshape(number * columns, model_width),
        head_weight,
        (((1,), (1,)), ((), ())),
        preferred_element_type=jnp.float32,
    )
    portion_targets = targets.reshape(-1)
    part_sum, part_pick = label_terms(logits, portion_targets, first_row)
    token_stats = jnp.stack(
        [part_sum.reshape(number, columns), part_pick.reshape(number, columns)], axis=1
    )
    partition = token_stats[:, 0]
    picked = token_stats[:, 1]
    own_cols = columns // groups
    row_start = data_index * sub_seq
    col_start = vocab_index * own_cols
    ref_full = lax.dynamic_update_slice(
        jnp.zeros((seq_total, columns), jnp.float32), ref_logps, (row_start, col_start)
    )
    partition, picked, ref_all = lax.psum((partition, picked, ref_full), ("dp", "vocab"))
    token_logps = picked - jnp.log(partition)
    differences = weights_mask * (token_logps - ref_all)
    logratio = jnp.sum(differences[:, :length], axis=1)
    kl_terms = jnp.sum(differences[:, length:], axis=1)
    losses = kto_losses(logratio, jnp.sum(kl_terms), seq_total, all_desirable)
    own_logps = lax.dynamic_slice(token_logps, (row_start, col_start), (sub_seq, own_cols))
    own_losses = lax.dynamic_slice_in_dim(losses, row_start, sub_seq, 0)
    return (own_logps, own_losses, jnp.mean(losses))


def solution(mesh):
    in_specs = (
        P("dp", None, "vocab"),
        P("dp", None, "vocab"),
        P(("dp", "vocab"), None),
        P("dp", None),
        P("dp", None),
        P("dp"),
        P("dp"),
        P("dp", "vocab"),
    )
    out_specs = (P("dp", "vocab"), P("dp"), P())
    return jax.shard_map(
        on_device, mesh=mesh, in_specs=in_specs, out_specs=out_specs, check_vma=False
    )
```

profile of v0, /device:TPU:0, one launch (start us, length us, event | category | flops | bytes accessed | tf_op | source)
XLA Modules:
  0.0 153.6 jit_solution(2589287121122592298)
XLA Ops:
  7.2 0.8 pad_maximum_fusion
  8.0 0.2 copy.14
  8.2 23.7 %all_gather.20 = bf16[1,64,3584]{1,0,2:T(2,128)(2,1)S(1)} all-gather(bf16[1,64,448]{1,0,2:T(2,128)(2,1)S(1)} %copy.14), channel_id=1, replica_groups=mesh['dp'=4,'vocab'=8] {'vocab'}, dimensions={2}, use_global_device_ids=true | all-gather | bytes 516096 | tf_op jit(solution)/shard_map/all_gather | solution.py:46
  31.8 3.1 %copy.15 = bf16[1,64,3584]{2,1,0:T(8,128)(2,1)} copy(bf16[1,64,3584]{1,0,2:T(2,128)(2,1)S(1)} %all_gather.20) | data formatting | bytes 917504 | tf_op jit(solution)/shard_map/all_gather | solution.py:46
  36.2 1.2 dynamic-slice
  37.5 0.8 dynamic-update-slice
  38.3 0.8 dynamic-update-slice.1
  39.0 7.4 %all-reduce.2 = (s32[4]{0:T(128)S(1)}, s32[4]{0:T(128)S(1)}) all-reduce(s32[4]{0:T(128)S(1)} %dynamic-update-slice, s32[4]{0:T(128)S(1)} %dynamic-update-slice.1), channel_id=1, replica_groups=mesh['dp'=4,'vocab'=8] {'dp'}, use_global_device_ids=true, to_apply=%add | all-reduce | flops 8 | bytes 64
  46.4 7.9 %all-gather.1 = s32[4,1,32]{2,1,0:T(1,128)S(1)} all-gather(s32[1,1,32]{2,1,0:T(1,128)} %bitcast.17), channel_id=1, replica_groups=mesh['dp'=4,'vocab'=8] {'dp'}, dimensions={0}, use_global_device_ids=true | all-gather | bytes 640 | tf_op jit(solution)/shard_map/all_gather | solution.py:37
  54.3 0.6 gather_fusion.1
  54.9 7.2 %all-gather = s32[4,1,32]{2,1,0:T(1,128)S(1)} all-gather(s32[1,1,32]{2,1,0:T(1,128)} %bitcast.18), channel_id=1, replica_groups=mesh['dp'=4,'vocab'=8] {'dp'}, dimensions={0}, use_global_device_ids=true | all-gather | bytes 640 | tf_op jit(solution)/shard_map/all_gather | solution.py:36
  62.1 0.6 gather_fusion
  62.8 0.1 min.12
  62.8 0.8 dynamic_update_slice.3
  63.7 4.1 %all-gather.4.cloned.1.call-done = bf16[4,64,3584]{2,1,0:T(8,128)(2,1)} async-done(((bf16[1,64,3584]{2,1,0:T(8,128)(2,1)}), bf16[4,64,3584]{2,1,0:T(8,128)(2,1)}) %all-gather.4.cloned.1.call-update) | async-done | bytes 1835024 | tf_op jit(solution)/shard_map/all_gather | solution.py:47
  67.7 25.9 %exponential_reduce_fusion = (f32[256]{0:T(256)S(1)}, f32[256,8000]{0,1:T(8,128)}) fusion(bf16[256,3584]{1,0:T(8,128)(2,1)} %bitcast.19, bf16[8000,3584]{1,0:T(8,128)(2,1)} %param.10), kind=kOutput, calls=%fused_computation.3 | convolution fusion | flops 14682112000 | bytes 67372032 | tf_op jit(solution)/shard_map/dot_general | solution.py:49
  93.6 9.0 %gather_fusion.2 = f32[256]{0:T(256)S(1)} fusion(f32[256,8000]{0,1:T(8,128)} %get-tuple-element.15, s32[256]{0:T(256)S(1)} %bitcast.11), kind=kCustom, calls=%fused_computation.2 | custom fusion | bytes 4096 | tf_op jit(solution)/shard_map/jit(take_along_axis)/gather | solution.py:15
  102.6 0.1 gather.14
  102.7 0.1 select_select_fusion
  102.8 38.9 %all-reduce.3 = (f32[4,64]{1,0:T(4,128)S(1)}, f32[4,64]{1,0:T(4,128)S(1)}, f32[4,64]{1,0:T(4,128)S(1)}) all-reduce(f32[4,64]{1,0:T(4,128)S(1)} %select_select_fusion, f32[4,64]{1,0:T(4,128)S(1)} %squeeze_stack_reshape.4, f32[4,64]{1,0:T(4,128)S(1)} %dynamic_update_slice.3), channel_id=1, replica_groups=mesh['dp'=4,'vocab'=8] {'dp','vocab'}, use_global_device_ids=true, to_apply=%region_0.1 | all-reduce | flops 768 | bytes 6144 | tf_op jit(solution)/shard_map/psum | solution.py:68
  141.8 0.6 dynamic_slice.6
  142.4 0.7 slice_reduce_fusion
  143.7 0.6 fusion.4
  144.4 0.6 dynamic_slice.7
  (14 shorter events, 0.3 us)
Async XLA Ops:
  7.2 60.6 %all-gather.4.cloned.1.call-start = ((), (), s32[]{:S(2)}) async-start(), calls=%async_computation | async-start | bytes 2293760 | tf_op jit(solution)/shard_map/all_gather | solution.py:47
Sparse Core Ops, SparseCore 0:
  35.1 32.6 all-gather.3
where the time goes:
time: 154 us
  blocking collectives  85.1 us (55%)
  matrix products  25.9 us (17%)
  local copies, waits for them, and re-layouts  18.3 us (12%)
  between operations  17.8 us (12%)
  waiting for transfers between devices  4.07 us (3%)
  other arithmetic  2.34 us (2%)
    psum x1, blocking collectives, on_device(): lax.psum((partition, picked, ref_full), ('dp', 'vocab'))  38.9 us
    dot_general x1, matrix products, on_device(): lax.dot_general(portion.reshape(number * columns, model_width), head_weig...  25.9 us
    all_gather x1, blocking collectives, on_device(): whole_rows = lax.all_gather(combined, 'vocab', axis=2, tiled=True)  23.7 us
    gather x2, local copies, waits for them, and re-layouts, label_terms(): picked = jnp.take_along_axis(logits, clipped[:, None], axis=1)[:, 0]  9.07 us
    all_gather x1, blocking collectives, on_device(): lax.all_gather(token_mask, 'dp', axis=0, tiled=True)  7.92 us
    unnamed x1, blocking collectives  7.39 us
    all_gather x1, blocking collectives, on_device(): lax.all_gather(labels, 'dp', axis=0, tiled=True)  7.23 us
    all_gather x1, waiting for transfers between devices, on_device(): portion = lax.all_gather(whole_rows, 'dp', axis=0, tiled=True)  4.05 us
  transfers between devices with their start and end apart: 1, of which 1 were waited for; matrix products, arithmetic and copies ran while one was open for 3% of the time, Pallas kernels for 0%

commit v1 on v0

--- a/solution.py
+++ b/solution.py
@@ -65,7 +65,7 @@
     ref_full = lax.dynamic_update_slice(
         jnp.zeros((seq_total, columns), jnp.float32), ref_logps, (row_start, col_start)
     )
-    partition, picked, ref_all = lax.psum((partition, picked, ref_full), ("dp", "vocab"))
+    partition, picked, ref_all = lax.psum(lax.psum((partition, picked, ref_full), "vocab"), "dp")
     token_logps = picked - jnp.log(partition)
     differences = weights_mask * (token_logps - ref_all)
     logratio = jnp.sum(differences[:, :length], axis=1)

time: 154 us -> 141 us (0.916)
  blocking collectives: 85.1 us -> 71.9 us
    psum x1 -> x2, blocking collectives: 38.9 us -> 25.7 us  [the longest x1 15.1 us: on_device(): lax.psum((partition, picked, ref_full), 'vocab')]
where the time goes in v1:
time: 141 us; the launch traced here: 140 us
  blocking collectives  71.9 us (51%)
  matrix products  25.9 us (18%)
  local copies, waits for them, and re-layouts  18.3 us (13%)
  between operations  17.8 us (13%)
  waiting for transfers between devices  4.07 us (3%)
  other arithmetic  2.35 us (2%)
    dot_general x1, matrix products, on_device(): lax.dot_general(portion.reshape(number * columns, model_width), head_weig...  25.9 us
    all_gather x1, blocking collectives, on_device(): whole_rows = lax.all_gather(combined, 'vocab', axis=2, tiled=True)  23.7 us
    psum x1, blocking collectives, on_device(): lax.psum((partition, picked, ref_full), 'vocab')  15.1 us
    psum x1, blocking collectives, on_device(): lax.psum(lax.psum((partition, picked, ref_full), 'vocab'), 'dp')  10.6 us
    gather x2, local copies, waits for them, and re-layouts, label_terms(): picked = jnp.take_along_axis(logits, clipped[:, None], axis=1)[:, 0]  9.07 us
    all_gather x1, blocking collectives, on_device(): lax.all_gather(token_mask, 'dp', axis=0, tiled=True)  7.92 us
    unnamed x1, blocking collectives  7.39 us
    all_gather x1, blocking collectives, on_device(): lax.all_gather(labels, 'dp', axis=0, tiled=True)  7.23 us
  transfers between devices with their start and end apart: 1, of which 1 were waited for; matrix products, arithmetic and copies ran while one was open for 3% of the time, Pallas kernels for 0%

profile of v1, /device:TPU:0, one launch (start us, length us, event | category | flops | bytes accessed | tf_op | source)
XLA Modules:
  0.0 140.3 jit_solution(2754930158683218777)
XLA Ops:
  7.2 0.8 pad_maximum_fusion
  8.0 0.2 copy.14
  8.2 23.7 %all_gather.20 = bf16[1,64,3584]{1,0,2:T(2,128)(2,1)S(1)} all-gather(bf16[1,64,448]{1,0,2:T(2,128)(2,1)S(1)} %copy.14), channel_id=1, replica_groups=mesh['dp'=4,'vocab'=8] {'vocab'}, dimensions={2}, use_global_device_ids=true | all-gather | bytes 516096 | tf_op jit(solution)/shard_map/all_gather | solution.py:46
  31.8 3.1 %copy.15 = bf16[1,64,3584]{2,1,0:T(8,128)(2,1)} copy(bf16[1,64,3584]{1,0,2:T(2,128)(2,1)S(1)} %all_gather.20) | data formatting | bytes 917504 | tf_op jit(solution)/shard_map/all_gather | solution.py:46
  36.2 1.2 dynamic-slice
  37.5 0.8 dynamic-update-slice
  38.3 0.8 dynamic-update-slice.1
  39.0 7.4 %all-reduce.2 = (s32[4]{0:T(128)S(1)}, s32[4]{0:T(128)S(1)}) all-reduce(s32[4]{0:T(128)S(1)} %dynamic-update-slice, s32[4]{0:T(128)S(1)} %dynamic-update-slice.1), channel_id=1, replica_groups=mesh['dp'=4,'vocab'=8] {'dp'}, use_global_device_ids=true, to_apply=%add | all-reduce | flops 8 | bytes 64
  46.4 7.9 %all-gather.1 = s32[4,1,32]{2,1,0:T(1,128)S(1)} all-gather(s32[1,1,32]{2,1,0:T(1,128)} %bitcast.17), channel_id=1, replica_groups=mesh['dp'=4,'vocab'=8] {'dp'}, dimensions={0}, use_global_device_ids=true | all-gather | bytes 640 | tf_op jit(solution)/shard_map/all_gather | solution.py:37
  54.3 0.6 gather_fusion.1
  54.9 7.2 %all-gather = s32[4,1,32]{2,1,0:T(1,128)S(1)} all-gather(s32[1,1,32]{2,1,0:T(1,128)} %bitcast.18), channel_id=1, replica_groups=mesh['dp'=4,'vocab'=8] {'dp'}, dimensions={0}, use_global_device_ids=true | all-gather | bytes 640 | tf_op jit(solution)/shard_map/all_gather | solution.py:36
  62.1 0.6 gather_fusion
  62.8 0.1 min.12
  62.8 0.8 dynamic_update_slice.3
  63.7 4.1 %all-gather.4.cloned.1.call-done = bf16[4,64,3584]{2,1,0:T(8,128)(2,1)} async-done(((bf16[1,64,3584]{2,1,0:T(8,128)(2,1)}), bf16[4,64,3584]{2,1,0:T(8,128)(2,1)}) %all-gather.4.cloned.1.call-update) | async-done | bytes 1835024 | tf_op jit(solution)/shard_map/all_gather | solution.py:47
  67.7 25.9 %exponential_reduce_fusion = (f32[256]{0:T(256)S(1)}, f32[256,8000]{0,1:T(8,128)}) fusion(bf16[256,3584]{1,0:T(8,128)(2,1)} %bitcast.19, bf16[8000,3584]{1,0:T(8,128)(2,1)} %param.10), kind=kOutput, calls=%fused_computation.3 | convolution fusion | flops 14682112000 | bytes 67372032 | tf_op jit(solution)/shard_map/dot_general | solution.py:49
  93.6 9.0 %gather_fusion.2 = f32[256]{0:T(256)S(1)} fusion(f32[256,8000]{0,1:T(8,128)} %get-tuple-element.18, s32[256]{0:T(256)S(1)} %bitcast.11), kind=kCustom, calls=%fused_computation.2 | custom fusion | bytes 4096 | tf_op jit(solution)/shard_map/jit(take_along_axis)/gather | solution.py:15
  102.7 0.1 select_select_fusion
  102.8 15.1 %all-reduce.3 = (f32[4,64]{1,0:T(4,128)S(1)}, f32[4,64]{1,0:T(4,128)S(1)}, f32[4,64]{1,0:T(4,128)S(1)}) all-reduce(f32[4,64]{1,0:T(4,128)S(1)} %select_select_fusion, f32[4,64]{1,0:T(4,128)S(1)} %squeeze_stack_reshape.4, f32[4,64]{1,0:T(4,128)S(1)} %dynamic_update_slice.3), channel_id=1, replica_groups=mesh['dp'=4,'vocab'=8] {'vocab'}, use_global_device_ids=true, to_apply=%region_0.1 | all-reduce | flops 768 | bytes 6144 | tf_op jit(solution)/shard_map/psum | solution.py:68
  117.9 10.6 %all-reduce.4 = (f32[4,64]{1,0:T(4,128)S(1)}, f32[4,64]{1,0:T(4,128)S(1)}, f32[4,64]{1,0:T(4,128)S(1)}) all-reduce(f32[4,64]{1,0:T(4,128)S(1)} %get-tuple-element.7, f32[4,64]{1,0:T(4,128)S(1)} %get-tuple-element.8, f32[4,64]{1,0:T(4,128)S(1)} %get-tuple-element.9), channel_id=1, replica_groups=mesh['dp'=4,'vocab'=8] {'dp'}, use_global_device_ids=true, to_apply=%region_1.2 | all-reduce | flops 768 | bytes 6144 | tf_op jit(solution)/shard_map/psum | solution.py:68
  128.6 0.6 dynamic_slice.6
  129.2 0.7 slice_reduce_fusion
  130.5 0.6 fusion.4
  131.1 0.6 dynamic_slice.7
  (15 shorter events, 0.4 us)
Async XLA Ops:
  7.2 60.6 %all-gather.4.cloned.1.call-start = ((), (), s32[]{:S(2)}) async-start(), calls=%async_computation | async-start | bytes 2293760 | tf_op jit(solution)/shard_map/all_gather | solution.py:47
Sparse Core Ops, SparseCore 0:
  35.1 32.6 all-gather.3
